TPU v7x, 32 devices: a whole 2x2x4 slice. The times are simulated.
32 devices in a mesh: rows: 16 (over z, y, x), cols: 2 (over core).
Axes of the slice: x: 2, y: 2, z: 4, core: 2. Of those that a mesh axis runs over, the one named last changes fastest.
Arguments:
- embeddings: bfloat16 [49152, 1536], P('rows'), may hold values from -43 to 43, as said below
- start_basis: float32 [1536, 256], P(None, 'cols'), may hold values from -6 to 6
Outputs:
- projected: bfloat16 [49152, 256], P('rows', 'cols')
- basis: float32 [1536, 256], P(None, 'cols')
Inputs may be any that keep to these rules, and one draw needn't show every extreme that they name: `embeddings`: rows are noisy vectors around offsets that differ between aligned blocks of rows, with per-column spreads that differ by a factor of up to four.
All inputs are finite; a program needn't handle non-finite values.
Results may differ from a plain program's by a relative error of at most 0.025.
Values may be sent and summed in bfloat16 or wider, within the bound.
A program may use at most 64 MiB of HBM per device.

v0:
```python
import jax
import jax.numpy as jnp
from jax import lax
from jax.sharding import PartitionSpec as P

K = 256
ITERS = 3


def shards(embeddings, start_basis):
    local_rows = embeddings.shape[0]
    col_block = start_basis.shape[1]
    col_start = lax.axis_index("cols") * col_block
    col_mean = lax.psum(jnp.sum(embeddings, axis=0, dtype=jnp.float32), "rows")
    col_mean = col_mean / (local_rows * lax.axis_size("rows"))
    basis = start_basis
    for sweep_index in range(ITERS):
        basis_bf = basis.astype(jnp.bfloat16)
        raw_proj = jnp.dot(embeddings, basis_bf, preferred_element_type=jnp.float32)
        offset = jnp.dot(col_mean, basis_bf.astype(jnp.float32), precision=lax.Precision.HIGHEST)
        shifted = (raw_proj - offset[None, :]).astype(jnp.bfloat16)
        local_sums = jnp.sum(shifted, axis=0, dtype=jnp.float32)
        partial_products = lax.dot_general(
            embeddings, shifted, (((0,), (0,)), ((), ())), preferred_element_type=jnp.float32
        )
        summed, col_sums = lax.psum((partial_products, local_sums), "rows")
        products = summed - col_mean[:, None] * col_sums[None, :]
        full_products = lax.all_gather(
            products.astype(jnp.bfloat16), "cols", axis=1, tiled=True
        ).astype(products.dtype)
        gram_matrix = jnp.dot(full_products.T, full_products, precision=lax.Precision.HIGHEST)
        lower = jnp.linalg.cholesky(gram_matrix)
        solved = lax.linalg.triangular_solve(
            lower, full_products, left_side=False, lower=True, transpose_a=True
        )
        basis = lax.dynamic_slice_in_dim(solved, col_start, col_block, 1)
    centered = embeddings.astype(jnp.float32) - col_mean[None, :]
    unit = (centered * lax.rsqrt(jnp.sum(centered * centered, axis=1, keepdims=True) + 1.0)).astype(
        jnp.bfloat16
    )
    coords = jnp.dot(unit, basis.astype(jnp.bfloat16), preferred_element_type=jnp.float32)
    squares = lax.psum(jnp.sum(coords * coords, axis=1), "cols")
    scaled = coords * lax.rsqrt(squares[:, None] / K + 0.0001)
    return (scaled.astype(jnp.bfloat16), basis)


def solution(mesh):
    in_specs = (P("rows", None), P(None, "cols"))
    out_specs = (P("rows", "cols"), P(None, "cols"))
    return jax.shard_map(shards, mesh=mesh, in_specs=in_specs, out_specs=out_specs, check_vma=False)
```

profile of v0, /device:TPU:0, one launch (start us, length us, event | category | flops | bytes accessed | tf_op | source)
XLA Modules:
  0.0 638.1 jit_solution(6976199507858413870)
XLA Ops:
  7.2 5.1 convert_reduce_fusion
  12.3 44.0 %psum.56 = f32[1536]{0:T(1024)S(1)} all-reduce(f32[1536]{0:T(1024)S(1)} %convert_reduce_fusion), channel_id=1, replica_groups=mesh['rows'=16,'cols'=2] {'rows'}, use_global_device_ids=true, to_apply=%region_1.0 | all-reduce | flops 1536 | bytes 12288 | tf_op jit(solution)/shard_map/psum | solution.py:14
  56.6 6.3 convert_reduce_fusion.3
  63.0 6.0 convolution_bitcast_fusion.2
  69.0 36.9 %psum.58 = f32[128]{0:T(128)S(1)} all-reduce(f32[128]{0:T(128)S(1)} %get-tuple-element.71), channel_id=1, replica_groups=mesh['rows'=16,'cols'=2] {'rows'}, use_global_device_ids=true, to_apply=%region_5.6 | all-reduce | flops 128 | bytes 1024 | tf_op jit(solution)/shard_map/psum | solution.py:26
  105.9 69.9 %all-reduce.5.cloned.1.call-done = f32[1536,128]{0,1:T(8,128)} async-done(((f32[1536,128]{0,1:T(8,128)}), f32[1536,128]{0,1:T(8,128)}) %all-reduce.5.cloned.1.call-update) | async-done | bytes 786448 | tf_op jit(solution)/shard_map/psum | solution.py:26
  175.8 1.3 subtract_convert_fusion.2
  177.1 2.5 all_gather.9
  180.4 11.7 %cholesky.172 = f32[128,128]{1,0:T(8,128)S(1)} custom-call(f32[128,128]{1,0:T(8,128)S(1)} %cholesky.270), custom_call_target="Cholesky" | custom-call | tf_op jit(solution)/shard_map/jit(cholesky)/cholesky | solution.py:32
  192.2 9.8 %custom-call.15 = f32[1,128,128]{1,2,0:T(8,128)S(1)} custom-call(f32[1,128,128]{2,1,0:T(8,128)S(1)} %get-tuple-element.70), custom_call_target="InvertDiagBlocksLowerTriangular" | custom-call | tf_op jit(solution)/shard_map/jit(cholesky)/cholesky | solution.py:32
  202.5 11.7 %cholesky.189 = f32[128,128]{1,0:T(8,128)S(1)} custom-call(f32[128,128]{1,0:T(8,128)S(1)} %convolution_subtract_fusion.8), custom_call_target="Cholesky" | custom-call | tf_op jit(solution)/shard_map/jit(cholesky)/cholesky | solution.py:32
  214.3 0.7 compare_reduce_fusion.4
  216.4 4.3 while.6
  216.7 0.6 fusion.94
  217.3 1.4 bitcast_dynamic-update-slice_fusion.6
  218.7 0.6 fusion.94
  219.3 1.4 bitcast_dynamic-update-slice_fusion.6
  220.8 19.7 %custom-call.16 = f32[2,128,128]{1,2,0:T(8,128)S(1)} custom-call(f32[2,128,128]{2,1,0:T(8,128)S(1)} %get-tuple-element.24), custom_call_target="InvertDiagBlocksLowerTriangular" | custom-call | tf_op jit(solution)/shard_map/triangular_solve/custom-call.0 | solution.py:33
  240.5 0.8 fusion.20
  241.3 0.8 convolution_subtract_fusion.5
  242.2 0.9 fusion.36
  243.6 7.1 %convert_reduce_fusion.2 = (f32[128]{0:T(128)S(1)}, bf16[128,3072]{1,0:T(8,128)(2,1)S(1)}) fusion(f32[128]{0:T(128)S(1)} %convolution_bitcast_fusion.4, bf16[1536,128]{0,1:T(8,128)(2,1)S(1)} %fusion.15, bf16[3072,1536]{1,0:T(8,128)(2,1)} %param.5), kind=kOutput, calls=%fused_computation.36 | convolution fusion | flops 1209532288 | bytes 10617856 | tf_op jit(solution)/shard_map/dot_general | solution.py:19
  250.7 2.3 convolution_bitcast_fusion.1
  253.1 39.9 %psum.60 = f32[128]{0:T(128)S(1)} all-reduce(f32[128]{0:T(128)S(1)} %get-tuple-element.75), channel_id=1, replica_groups=mesh['rows'=16,'cols'=2] {'rows'}, use_global_device_ids=true, to_apply=%region_12.15 | all-reduce | flops 128 | bytes 1024 | tf_op jit(solution)/shard_map/psum | solution.py:26
  292.9 70.4 %all-reduce.7.cloned.1.call-done = f32[1536,128]{0,1:T(8,128)} async-done(((f32[1536,128]{0,1:T(8,128)}), f32[1536,128]{0,1:T(8,128)}) %all-reduce.7.cloned.1.call-update) | async-done | bytes 786448 | tf_op jit(solution)/shard_map/psum | solution.py:26
  363.4 1.3 subtract_convert_fusion.1
  364.6 2.8 all_gather.10
  368.2 11.7 %cholesky.206 = f32[128,128]{1,0:T(8,128)S(1)} custom-call(f32[128,128]{1,0:T(8,128)S(1)} %cholesky.273), custom_call_target="Cholesky" | custom-call | tf_op jit(solution)/shard_map/jit(cholesky)/cholesky | solution.py:32
  380.0 9.8 %custom-call.17 = f32[1,128,128]{1,2,0:T(8,128)S(1)} custom-call(f32[1,128,128]{2,1,0:T(8,128)S(1)} %get-tuple-element.66), custom_call_target="InvertDiagBlocksLowerTriangular" | custom-call | tf_op jit(solution)/shard_map/jit(cholesky)/cholesky | solution.py:32
  390.3 11.7 %cholesky.223 = f32[128,128]{1,0:T(8,128)S(1)} custom-call(f32[128,128]{1,0:T(8,128)S(1)} %convolution_subtract_fusion.7), custom_call_target="Cholesky" | custom-call | tf_op jit(solution)/shard_map/jit(cholesky)/cholesky | solution.py:32
  402.0 0.7 compare_reduce_fusion.2
  402.8 0.6 compare_reduce_fusion.3
  404.8 4.3 while.7
  405.0 0.6 fusion.95
  405.6 1.4 bitcast_dynamic-update-slice_fusion.7
  407.0 0.6 fusion.95
  407.6 1.4 bitcast_dynamic-update-slice_fusion.7
  409.1 19.7 %custom-call.18 = f32[2,128,128]{1,2,0:T(8,128)S(1)} custom-call(f32[2,128,128]{2,1,0:T(8,128)S(1)} %get-tuple-element.25), custom_call_target="InvertDiagBlocksLowerTriangular" | custom-call | tf_op jit(solution)/shard_map/triangular_solve/custom-call.0 | solution.py:33
  428.8 0.8 fusion.18
  429.6 0.8 convolution_subtract_fusion.4
  430.5 0.8 fusion.32
  431.9 7.1 %convert_reduce_fusion.1 = (f32[128]{0:T(128)S(1)}, bf16[128,3072]{1,0:T(8,128)(2,1)S(1)}) fusion(f32[128]{0:T(128)S(1)} %convolution_bitcast_fusion.3, bf16[1536,128]{0,1:T(8,128)(2,1)S(1)} %fusion.13, bf16[3072,1536]{1,0:T(8,128)(2,1)} %param.5), kind=kOutput, calls=%fused_computation.35 | convolution fusion | flops 1209532288 | bytes 10617856 | tf_op jit(solution)/shard_map/dot_general | solution.py:19
  439.0 2.3 convolution_bitcast_fusion
  441.3 6.2 fusion.2
  447.5 39.8 %psum.62 = f32[128]{0:T(128)S(1)} all-reduce(f32[128]{0:T(128)S(1)} %get-tuple-element.79), channel_id=1, replica_groups=mesh['rows'=16,'cols'=2] {'rows'}, use_global_device_ids=true, to_apply=%region_15.18 | all-reduce | flops 128 | bytes 1024 | tf_op jit(solution)/shard_map/psum | solution.py:26
  487.3 64.2 %all-reduce.9.cloned.1.call-done = f32[1536,128]{0,1:T(8,128)} async-done(((f32[1536,128]{0,1:T(8,128)}), f32[1536,128]{0,1:T(8,128)}) %all-reduce.9.cloned.1.call-update) | async-done | bytes 786448 | tf_op jit(solution)/shard_map/psum | solution.py:26
  551.5 1.3 subtract_convert_fusion
  552.8 2.6 all_gather.11
  556.2 11.7 %cholesky.240 = f32[128,128]{1,0:T(8,128)S(1)} custom-call(f32[128,128]{1,0:T(8,128)S(1)} %cholesky.276), custom_call_target="Cholesky" | custom-call | tf_op jit(solution)/shard_map/jit(cholesky)/cholesky | solution.py:32
  567.9 9.8 %custom-call.19 = f32[1,128,128]{1,2,0:T(8,128)S(1)} custom-call(f32[1,128,128]{2,1,0:T(8,128)S(1)} %get-tuple-element.62), custom_call_target="InvertDiagBlocksLowerTriangular" | custom-call | tf_op jit(solution)/shard_map/jit(cholesky)/cholesky | solution.py:32
  578.2 11.7 %cholesky.257 = f32[128,128]{1,0:T(8,128)S(1)} custom-call(f32[128,128]{1,0:T(8,128)S(1)} %convolution_subtract_fusion.6), custom_call_target="Cholesky" | custom-call | tf_op jit(solution)/shard_map/jit(cholesky)/cholesky | solution.py:32
  590.0 0.7 compare_reduce_fusion
  590.7 0.6 compare_reduce_fusion.1
  592.7 4.4 while.8
  593.6 1.4 bitcast_dynamic-update-slice_fusion.8
  595.7 1.4 bitcast_dynamic-update-slice_fusion.8
  597.1 19.7 %custom-call.20 = f32[2,128,128]{1,2,0:T(8,128)S(1)} custom-call(f32[2,128,128]{2,1,0:T(8,128)S(1)} %get-tuple-element.26), custom_call_target="InvertDiagBlocksLowerTriangular" | custom-call | tf_op jit(solution)/shard_map/triangular_solve/custom-call.0 | solution.py:33
  616.8 0.8 fusion.16
  617.6 0.8 convolution_subtract_fusion.3
  618.5 0.8 fusion.28
  619.5 1.1 copy.8
  620.7 6.0 multiply_reduce_fusion
  626.7 3.3 psum.63
  630.1 1.2 copy.7
  (79 shorter events, 7.3 us)
Async XLA Ops:
  7.2 49.2 %copy-start = (f32[1536,128]{1,0:T(8,128)S(1)}, f32[1536,128]{1,0:T(8,128)}, u32[]{:S(2)}) copy-start(f32[1536,128]{1,0:T(8,128)} %param.6) | copy-start | bytes 2359300
  7.2 168.7 %all-reduce.5.cloned.1.call-start = ((), (), s32[]{:S(2)}) async-start(), calls=%async_computation | async-start | bytes 1572864 | tf_op jit(solution)/shard_map/psum | solution.py:26
  69.0 294.4 %all-reduce.7.cloned.1.call-start = ((), (), s32[]{:S(2)}) async-start(), calls=%async_computation.1 | async-start | bytes 1572864 | tf_op jit(solution)/shard_map/psum | solution.py:26
  180.4 70.3 %slice-start = ((s8[9437184]{0:T(1024)(128)(4,1)}), s8[1048576]{0:T(1024)(128)(4,1)S(1)}, s32[]{:S(2)}) async-start(s8[9437184]{0:T(1024)(128)(4,1)} %bitcast.130), calls=%async_computation.3 | async-start | bytes 2097152
  241.3 9.4 %slice-start.1 = ((s8[9437184]{0:T(1024)(128)(4,1)}), s8[4194304]{0:T(1024)(128)(4,1)S(1)}, s32[]{:S(2)}) async-start(s8[9437184]{0:T(1024)(128)(4,1)} %bitcast.130), calls=%async_computation.4 | async-start | bytes 8388608
  243.6 7.1 %slice-start.2 = ((s8[9437184]{0:T(1024)(128)(4,1)}), s8[4194304]{0:T(1024)(128)(4,1)S(1)}, s32[]{:S(2)}) async-start(s8[9437184]{0:T(1024)(128)(4,1)} %bitcast.130), calls=%async_computation.5 | async-start | bytes 8388608
  253.0 298.5 %all-reduce.9.cloned.1.call-start = ((), (), s32[]{:S(2)}) async-start(), calls=%async_computation.2 | async-start | bytes 1572864 | tf_op jit(solution)/shard_map/psum | solution.py:26
  368.1 70.8 %slice-start.3 = ((s8[9437184]{0:T(1024)(128)(4,1)}), s8[1048576]{0:T(1024)(128)(4,1)S(1)}, s32[]{:S(2)}) async-start(s8[9437184]{0:T(1024)(128)(4,1)} %bitcast.132), calls=%async_computation.6 | async-start | bytes 2097152
  429.6 9.4 %slice-start.4 = ((s8[9437184]{0:T(1024)(128)(4,1)}), s8[4194304]{0:T(1024)(128)(4,1)S(1)}, s32[]{:S(2)}) async-start(s8[9437184]{0:T(1024)(128)(4,1)} %bitcast.132), calls=%async_computation.7 | async-start | bytes 8388608
  431.9 7.1 %slice-start.5 = ((s8[9437184]{0:T(1024)(128)(4,1)}), s8[4194304]{0:T(1024)(128)(4,1)S(1)}, s32[]{:S(2)}) async-start(s8[9437184]{0:T(1024)(128)(4,1)} %bitcast.132), calls=%async_computation.8 | async-start | bytes 8388608
Sparse Core Ops, SparseCore 0:
  69.1 106.6 all-reduce.4
  253.1 110.1 all-reduce.6
  441.5 110.0 all-reduce.8
where the time goes:
time: 643 us; the launch traced here: 638 us
  waiting for transfers between devices  205 us (32%)
  other arithmetic  179 us (28%)
  blocking collectives  172 us (27%)
  matrix products  48.3 us (8%)
  between operations  18.6 us (3%)
  local copies, waits for them, and re-layouts  15.1 us (2%)
    psum x3, waiting for transfers between devices, shards(): summed, col_sums = lax.psum((partial_products, local_sums), 'rows')  205 us
    psum x3, blocking collectives, shards(): summed, col_sums = lax.psum((partial_products, local_sums), 'rows')  117 us
    another operation x20, other arithmetic, shards(): lower = jnp.linalg.cholesky(gram_matrix)  103 us
    another operation x8, other arithmetic, shards(): lax.linalg.triangular_solve(lower, full_products, left_side=False, lower=...  59.3 us
    psum x1, blocking collectives, shards(): col_mean = lax.psum(jnp.sum(embeddings, axis=0, dtype=jnp.float32), 'rows')  44 us
    dot_general x3, matrix products, shards(): raw_proj = jnp.dot(embeddings, basis_bf, preferred_element_type=jnp.float32)  20.5 us
  transfers between devices with their start and end apart: 3, of which 3 were waited for; matrix products, arithmetic and copies ran while one was open for 1% of the time, Pallas kernels for 0%

commit v1 on v0

v1 whole, which is shorter than its diff:
```python
import functools

import jax
import jax.numpy as jnp
from jax import lax
from jax.experimental import pallas as pl
from jax.experimental.pallas import tpu as pltpu
from jax.sharding import PartitionSpec as P

ITERS = 3
PARTS = 3
HI = lax.Precision.HIGHEST
F32 = jnp.float32
BF16 = jnp.bfloat16


def dot(a, b, ca, cb, precision=None):
    return lax.dot_general(a, b, (((ca,), (cb,)), ((), ())), precision=precision, preferred_element_type=F32)


def scatter_kernel(n, e_ref, w_ref, s_ref, acc, sums):
    step = pl.program_id(0)
    core = lax.axis_index("cols")
    t = acc.shape[1]

    @pl.when(step == 0)
    def _():
        acc[...] = jnp.zeros_like(acc)
        sums[...] = jnp.zeros_like(sums)

    e = e_ref[...]
    sums[...] += dot(jnp.ones((8, e.shape[0]), BF16), e, 1, 0)

    def block(slot, i, j):
        acc[slot] += dot(e[:, i * t:(i + 1) * t], e[:, j * t:(j + 1) * t], 0, 0)

    def finish(slot, i, j):
        si = sums[:, i * t:(i + 1) * t] * (1.0 / (8 * n))
        sj = sums[:, j * t:(j + 1) * t]
        w_ref[slot] = (acc[slot] - dot(si, sj, 0, 0, HI)).astype(w_ref.dtype)

    last = step == pl.num_programs(0) - 1
    for c, pairs in enumerate((((0, 0), (0, 1), (0, 2)), ((1, 1), (1, 2), (2, 2)))):
        @pl.when(core == c)
        def _(pairs=pairs):
            for slot, (i, j) in enumerate(pairs):
                block(slot, i, j)

            @pl.when(last)
            def _():
                for slot, (i, j) in enumerate(pairs):
                    finish(slot, i, j)

    @pl.when(last)
    def _():
        s_ref[...] = sums[...]


def scatter(e, rows=512):
    n, d = e.shape
    t = d // PARTS
    return pl.pallas_call(
        functools.partial(scatter_kernel, n),
        grid=(n // rows,),
        in_specs=[pl.BlockSpec((rows, d), lambda i: (i, 0))],
        out_specs=[pl.BlockSpec((PARTS, t, t), lambda i: (0, 0, 0)), pl.BlockSpec((8, d), lambda i: (0, 0))],
        out_shape=[jax.ShapeDtypeStruct((PARTS, t, t), BF16), jax.ShapeDtypeStruct((8, d), F32)],
        scratch_shapes=[pltpu.VMEM((PARTS, t, t), F32), pltpu.VMEM((8, d), F32)],
    )(e)


def inverse_factor(a_ref, k, b):
    sub = lax.broadcasted_iota(jnp.int32, (8, 2 * b), 0)
    eye = (lax.broadcasted_iota(jnp.int32, (b, b), 0) == lax.broadcasted_iota(jnp.int32, (b, b), 1)).astype(F32)
    for blk in range(k // b):
        lo, hi = blk * b, (blk + 1) * b
        aug = jnp.concatenate([a_ref[lo:hi, lo:hi], eye], axis=1)
        tiles = [aug[8 * t:8 * t + 8] for t in range(b // 8)]
        for j in range(b):
            tj, r = j // 8, j % 8
            cols = {t: jnp.broadcast_to(tiles[t][:, j:j + 1], (8, 2 * b)) for t in range(tj, b // 8)}
            row = tiles[tj][r:r + 1] * (1.0 / cols[tj][r:r + 1])
            for t in range(tj, b // 8):
                f = cols[t]
                if t == tj:
                    if r == 7:
                        continue
                    f = jnp.where(sub > r, f, 0.0)
                tiles[t] = tiles[t] - f * row
        aug = jnp.concatenate(tiles, axis=0)
        diag = jnp.sum(aug[:, :b] * eye, axis=1, keepdims=True)
        scale = lax.rsqrt(diag)
        scale = scale * (1.5 - 0.5 * diag * scale * scale)
        strip = dot(aug[:, b:] * scale, a_ref[lo:hi, :], 1, 0, HI)
        a_ref[lo:hi, :] = strip
        if hi < k:
            a_ref[hi:, :] -= dot(strip[:, hi:k], strip, 0, 0, HI)


def iterate_kernel(n, total, w_ref, s_ref, b_ref, out_ref, w, basis, mean, a):
    d, k = out_ref.shape
    t = d // PARTS
    for c, pairs in enumerate((((0, 0), (0, 1), (0, 2)), ((1, 1), (1, 2), (2, 2)))):
        for slot, (i, j) in enumerate(pairs):
            v = w_ref[c, slot]
            w[i * t:(i + 1) * t, j * t:(j + 1) * t] = v
            if i != j:
                w[j * t:(j + 1) * t, i * t:(i + 1) * t] = v.T
    s = s_ref[...]
    mean[...] = s * (1.0 / n) - jnp.sum(s, axis=0, keepdims=True) * (1.0 / total)
    basis[...] = b_ref[...]

    @pl.loop(0, ITERS)
    def _(_):
        bf = basis[...]
        m = mean[...]
        inner = dot(m, bf.astype(F32), 1, 0, HI) * float(n)
        products = dot(w[...], bf, 1, 0) + dot(m, inner, 0, 0, HI)
        a[:, :k] = dot(products, products, 0, 0, HI)
        a[:, k:] = (
            lax.broadcasted_iota(jnp.int32, (k, k), 0) == lax.broadcasted_iota(jnp.int32, (k, k), 1)
        ).astype(F32)
        inverse_factor(a, k, 64)
        new = dot(products, a[:, k:], 1, 1, HI)
        out_ref[...] = new
        basis[...] = new.astype(BF16)


def iterate(n, total, w, s, b):
    d, k = b.shape
    vm = pl.BlockSpec(memory_space=pltpu.VMEM)
    return pl.pallas_call(
        functools.partial(iterate_kernel, n, total),
        in_specs=[vm] * 3,
        out_specs=vm,
        out_shape=jax.ShapeDtypeStruct((d, k), F32),
        scratch_shapes=[
            pltpu.VMEM((d, d), BF16),
            pltpu.VMEM((d, k), BF16),
            pltpu.VMEM(s.shape, F32),
            pltpu.VMEM((k, 2 * k), F32),
        ],
    )(w, s, b)


def project_kernel(total, e_ref, s_ref, b_ref, o_ref, basis_ref, mean, bf):
    core = lax.axis_index("cols")
    h = o_ref.shape[1]

    @pl.when(pl.program_id(0) == 0)
    def _():
        mean[...] = jnp.sum(s_ref[...], axis=0, keepdims=True) * (1.0 / total)
        full = b_ref[...]
        bf[...] = full.astype(BF16)
        basis_ref[...] = jnp.where(core == 0, full[:, :h], full[:, h:])

    centered = e_ref[...].astype(F32) - mean[...]
    unit = (centered * lax.rsqrt(jnp.sum(centered * centered, axis=1, keepdims=True) + 1.0)).astype(BF16)
    coords = dot(unit, bf[...], 1, 0)
    k = coords.shape[1]
    scale = lax.rsqrt(jnp.sum(coords * coords, axis=1, keepdims=True) * (1.0 / k) + 0.0001)
    o_ref[...] = (jnp.where(core == 0, coords[:, :h], coords[:, h:]) * scale).astype(o_ref.dtype)


def project(total, e, s, b, h, rows=512):
    n, d = e.shape
    k = b.shape[1]
    return pl.pallas_call(
        functools.partial(project_kernel, total),
        grid=(n // rows,),
        in_specs=[
            pl.BlockSpec((rows, d), lambda i: (i, 0)),
            pl.BlockSpec(s.shape, lambda i: (0, 0)),
            pl.BlockSpec((d, k), lambda i: (0, 0)),
        ],
        out_specs=[pl.BlockSpec((rows, h), lambda i: (i, 0)), pl.BlockSpec((d, h), lambda i: (0, 0))],
        out_shape=[jax.ShapeDtypeStruct((n, h), BF16), jax.ShapeDtypeStruct((d, h), F32)],
        scratch_shapes=[pltpu.VMEM((1, d), F32), pltpu.VMEM((d, k), BF16)],
    )(e, s, b)


def shards(embeddings, start_basis):
    n, d = embeddings.shape
    total = n * lax.axis_size("rows")
    w, s = scatter(embeddings)
    w = lax.psum(w, "rows")
    w = lax.all_gather(w, "cols", axis=0)
    s = lax.all_gather(s[0], "rows", axis=0)
    b = lax.all_gather(start_basis.astype(BF16), "cols", axis=1, tiled=True)
    basis = iterate(n, total, w, s, b)
    return project(total, embeddings, s, basis, start_basis.shape[1])


def solution(mesh):
    in_specs = (P("rows", None), P(None, "cols"))
    out_specs = (P("rows", "cols"), P(None, "cols"))
    return jax.shard_map(shards, mesh=mesh, in_specs=in_specs, out_specs=out_specs, check_vma=False)
```

time: 643 us -> 308 us (0.48)
  other arithmetic: 179 us -> 0.04 us
  blocking collectives: 172 us -> 41.9 us
  Pallas kernels: 0 us -> 129 us
  waiting for transfers between devices: 205 us -> 120 us
  matrix products: 48.3 us -> 0 us
  local copies, waits for them, and re-layouts: 15.1 us -> 1.45 us
    psum x5 -> x0, blocking collectives: 164 us -> none  [the longest x3 117 us: shards(): summed, col_sums = lax.psum((partial_products, local_sums), 'rows')]
    another operation x28 -> x0, other arithmetic: 163 us -> none  [the longest x20 103 us: shards(): lower = jnp.linalg.cholesky(gram_matrix)]
    pallas_call x0 -> x3, Pallas kernels: none -> 129 us  [the longest x1 106 us: iterate(): pl.pallas_call(functools.partial(iterate_kernel, n, total), in_specs=[vm]...]
    psum x3 -> x1, waiting for transfers between devices: 205 us -> 120 us  [shards(): w = lax.psum(w, 'rows')]
    dot_general x13 -> x0, matrix products: 39.3 us -> none  [the longest x3 20.5 us: shards(): raw_proj = jnp.dot(embeddings, basis_bf, preferred_element_type=jnp.float32)]
    all_gather x3 -> x2, blocking collectives: 7.9 us -> 41.9 us  [the longest x1 39.4 us: shards(): s = lax.all_gather(s[0], 'rows', axis=0)]
    another operation x28 -> x0, local copies, waits for them, and re-layouts: 12.3 us -> none  [the longest x22 12.3 us: shards(): lax.linalg.triangular_solve(lower, full_products, left_side=False, lower=...]
    reduce_sum x2 -> x0, other arithmetic: 11.3 us -> none  [the longest x1 6.19 us: shards(): jnp.sum(centered * centered, axis=1, keepdims=True) + 1.0]
  transfers between devices with their start and end apart: 3 -> 2, of which waited for: 3 -> 1; matrix products, arithmetic and copies ran while one was open for 1% -> 0% of each run, Pallas kernels for 0% -> 0%
where the time goes in v1:
time: 308 us; the launch traced here: 307 us
  Pallas kernels  129 us (42%)
  waiting for transfers between devices  120 us (39%)
  blocking collectives  41.9 us (14%)
  between operations  14.1 us (5%)
    psum x1, waiting for transfers between devices, shards(): w = lax.psum(w, 'rows')  120 us
    pallas_call x1, Pallas kernels, iterate(): pl.pallas_call(functools.partial(iterate_kernel, n, total), in_specs=[vm]...  106 us
    all_gather x1, blocking collectives, shards(): s = lax.all_gather(s[0], 'rows', axis=0)  39.4 us
    pallas_call x1, Pallas kernels, scatter(): pl.pallas_call(functools.partial(scatter_kernel, n), grid=(n // rows,), i...  13.7 us
    pallas_call x1, Pallas kernels, project(): pl.pallas_call(functools.partial(project_kernel, total), grid=(n // rows,...  10 us
  transfers between devices with their start and end apart: 2, of which 1 were waited for; matrix products, arithmetic and copies ran while one was open for 0% of the time, Pallas kernels for 0%

profile of v1, /device:TPU:0, one launch (start us, length us, event | category | flops | bytes accessed | tf_op | source)
XLA Modules:
  0.0 307.2 jit_solution(15289075663225709811)
XLA Ops:
  7.2 0.0 all-reduce.2.cloned.1.call-start
  7.2 13.7 %shard_map.41 = (bf16[3,512,512]{2,1,0:T(8,128)(2,1)}, f32[8,1536]{1,0:T(8,128)}) custom-call(bf16[3072,1536]{1,0:T(8,128)(2,1)} %e_ref.3), custom_call_target="tpu_custom_call" | custom-call | tf_op jit(solution)/shard_map/pallas_call | solution.py:62
  20.9 0.0 copy-start
  20.9 0.0 all-reduce.2.cloned.1.call-update
  20.9 0.0 all-gather.3.cloned.1.call-start
  21.0 120.2 %all-reduce.2.cloned.1.call-done = bf16[1,3,512,512]{3,2,1,0:T(8,128)(2,1)} async-done(((bf16[1,3,512,512]{3,2,1,0:T(8,128)(2,1)}), bf16[1,3,512,512]{3,2,1,0:T(8,128)(2,1)}) %all-reduce.2.cloned.1.call-update) | async-done | bytes 1572880 | tf_op jit(solution)/shard_map/psum | solution.py:186
  141.2 0.0 all-gather.3.cloned.1.call-update
  141.2 0.0 copy-done
  141.3 0.8 slice_bitcast_fusion
  142.1 39.4 %all-gather = f32[16,1,1536]{2,1,0:T(1,128)S(1)} all-gather(f32[1,1,1536]{2,1,0:T(1,128)S(1)} %slice_bitcast_fusion), channel_id=1, replica_groups=mesh['rows'=16,'cols'=2] {'rows'}, dimensions={0}, use_global_device_ids=true | all-gather | bytes 104448 | tf_op jit(solution)/shard_map/all_gather | solution.py:188
  181.5 0.6 copy.6
  182.1 2.5 all_gather.15.b_ref
  184.7 0.0 all-gather.3.cloned.1.call-done.w_ref
  184.7 105.7 %shard_map.42.b_ref = f32[1536,256]{1,0:T(8,128)} custom-call(bf16[2,3,512,512]{3,2,1,0:T(8,128)(2,1)} %all-gather.3.cloned.1.call-done.w_ref, f32[16,1536]{1,0:T(8,128)} %bitcast.7, bf16[1536,256]{1,0:T(8,128)(2,1)} %all_gather.15.b_ref), custom_call_target="tpu_custom_call" | custom-call | tf_op jit(solution)/shard_map/pallas_call | solution.py:132
  290.3 10.0 %shard_map.43 = (bf16[3072,128]{1,0:T(8,128)(2,1)}, f32[1536,128]{1,0:T(8,128)}) custom-call(bf16[3072,1536]{1,0:T(8,128)(2,1)} %e_ref.3, f32[16,1536]{1,0:T(8,128)} %bitcast.8, f32[1536,256]{1,0:T(8,128)} %shard_map.42.b_ref), custom_call_target="tpu_custom_call" | custom-call | tf_op jit(solution)/shard_map/pallas_call | solution.py:168
  (1 shorter events, 0.0 us)
Async XLA Ops:
  7.2 134.0 %all-reduce.2.cloned.1.call-start = ((), (), s32[]{:S(2)}) async-start(), calls=%async_computation | async-start | bytes 3145728 | tf_op jit(solution)/shard_map/psum | solution.py:186
  20.9 120.3 %copy-start = (f32[1536,128]{1,0:T(8,128)S(1)}, f32[1536,128]{1,0:T(8,128)}, u32[]{:S(2)}) copy-start(f32[1536,128]{1,0:T(8,128)} %param.3) | copy-start | bytes 2359300
  20.9 163.7 %all-gather.3.cloned.1.call-start = ((), (), s32[]{:S(2)}) async-start(), calls=%async_computation.1 | async-start | bytes 4718592 | tf_op jit(solution)/shard_map/all_gather | solution.py:187
Sparse Core Ops, SparseCore 0:
  21.0 120.1 all-reduce.1
  142.7 11.2 all-gather.2

commit v2 on v1

--- a/solution.py
+++ b/solution.py
@@ -9,6 +9,8 @@
 
 ITERS = 3
 PARTS = 3
+LANES = 128
+MESH = pl.DeviceIdType.MESH
 HI = lax.Precision.HIGHEST
 F32 = jnp.float32
 BF16 = jnp.bfloat16
@@ -37,7 +39,9 @@
     def finish(slot, i, j):
         si = sums[:, i * t:(i + 1) * t] * (1.0 / (8 * n))
         sj = sums[:, j * t:(j + 1) * t]
-        w_ref[slot] = (acc[slot] - dot(si, sj, 0, 0, HI)).astype(w_ref.dtype)
+        v = (acc[slot] - dot(si, sj, 0, 0, HI)).astype(w_ref.dtype)
+        for c in range(t // LANES):
+            w_ref[slot, c] = v[:, c * LANES:(c + 1) * LANES]
 
     last = step == pl.num_programs(0) - 1
     for c, pairs in enumerate((((0, 0), (0, 1), (0, 2)), ((1, 1), (1, 2), (2, 2)))):
@@ -53,7 +57,7 @@
 
     @pl.when(last)
     def _():
-        s_ref[...] = sums[...]
+        s_ref[...] = sums[0:1, :]
 
 
 def scatter(e, rows=512):
@@ -63,8 +67,14 @@
         functools.partial(scatter_kernel, n),
         grid=(n // rows,),
         in_specs=[pl.BlockSpec((rows, d), lambda i: (i, 0))],
-        out_specs=[pl.BlockSpec((PARTS, t, t), lambda i: (0, 0, 0)), pl.BlockSpec((8, d), lambda i: (0, 0))],
-        out_shape=[jax.ShapeDtypeStruct((PARTS, t, t), BF16), jax.ShapeDtypeStruct((8, d), F32)],
+        out_specs=[
+            pl.BlockSpec((PARTS, t // LANES, t, LANES), lambda i: (0, 0, 0, 0)),
+            pl.BlockSpec((1, d), lambda i: (0, 0)),
+        ],
+        out_shape=[
+            jax.ShapeDtypeStruct((PARTS, t // LANES, t, LANES), BF16),
+            jax.ShapeDtypeStruct((1, d), F32),
+        ],
         scratch_shapes=[pltpu.VMEM((PARTS, t, t), F32), pltpu.VMEM((8, d), F32)],
     )(e)
 
@@ -102,13 +112,13 @@
     t = d // PARTS
     for c, pairs in enumerate((((0, 0), (0, 1), (0, 2)), ((1, 1), (1, 2), (2, 2)))):
         for slot, (i, j) in enumerate(pairs):
-            v = w_ref[c, slot]
+            v = jnp.concatenate([w_ref[c, slot, l] for l in range(t // LANES)], axis=1)
             w[i * t:(i + 1) * t, j * t:(j + 1) * t] = v
             if i != j:
                 w[j * t:(j + 1) * t, i * t:(i + 1) * t] = v.T
-    s = s_ref[...]
+    s = s_ref[:, 0, :]
     mean[...] = s * (1.0 / n) - jnp.sum(s, axis=0, keepdims=True) * (1.0 / total)
-    basis[...] = b_ref[...]
+    basis[...] = jnp.concatenate([b_ref[0], b_ref[1]], axis=1)
 
     @pl.loop(0, ITERS)
     def _(_):
@@ -127,7 +137,7 @@
 
 
 def iterate(n, total, w, s, b):
-    d, k = b.shape
+    d, k = b.shape[1], 2 * b.shape[2]
     vm = pl.BlockSpec(memory_space=pltpu.VMEM)
     return pl.pallas_call(
         functools.partial(iterate_kernel, n, total),
@@ -137,7 +147,7 @@
         scratch_shapes=[
             pltpu.VMEM((d, d), BF16),
             pltpu.VMEM((d, k), BF16),
-            pltpu.VMEM(s.shape, F32),
+            pltpu.VMEM((s.shape[0], d), F32),
             pltpu.VMEM((k, 2 * k), F32),
         ],
     )(w, s, b)
@@ -149,7 +159,7 @@
 
     @pl.when(pl.program_id(0) == 0)
     def _():
-        mean[...] = jnp.sum(s_ref[...], axis=0, keepdims=True) * (1.0 / total)
+        mean[...] = jnp.sum(s_ref[:, 0, :], axis=0, keepdims=True) * (1.0 / total)
         full = b_ref[...]
         bf[...] = full.astype(BF16)
         basis_ref[...] = jnp.where(core == 0, full[:, :h], full[:, h:])
@@ -170,7 +180,7 @@
         grid=(n // rows,),
         in_specs=[
             pl.BlockSpec((rows, d), lambda i: (i, 0)),
-            pl.BlockSpec(s.shape, lambda i: (0, 0)),
+            pl.BlockSpec(s.shape, lambda i: (0, 0, 0)),
             pl.BlockSpec((d, k), lambda i: (0, 0)),
         ],
         out_specs=[pl.BlockSpec((rows, h), lambda i: (i, 0)), pl.BlockSpec((d, h), lambda i: (0, 0))],
@@ -179,14 +189,181 @@
     )(e, s, b)
 
 
+def factors(r):
+    z = 4 if r % 4 == 0 else 1
+    x = 1
+    while x * x < r // z:
+        x *= 2
+    return z, r // z // x, x
+
+
+def reduce_kernel(r, w_ref, s_ref, b_ref, wout, sout, bout, *scratch):
+    nz, ny, nx = factors(r)
+    plans = (("x", "y", "z"), ("y", "x", "z"))
+    size = {"x": nx, "y": ny, "z": nz}
+    stride = {"x": 1, "y": nx, "z": nx * ny}
+    scratch = list(scratch)
+    stage = [[scratch.pop(0) for _ in plan] for plan in plans]
+    held = [[scratch.pop(0) for _ in plan[:-1]] for plan in plans]
+    w_send, w_recv, s_send, s_recv, c_send, c_recv = scratch
+
+    me = lax.axis_index("rows")
+    core = lax.axis_index("cols")
+    at = {a: lax.rem(me // stride[a], size[a]) for a in size}
+    partner = {"cols": 1 - core}
+
+    def peer(a, k):
+        p = lax.rem(at[a] + k, size[a])
+        return p, {"rows": me + (p - at[a]) * stride[a]}
+
+    barrier = pltpu.get_barrier_semaphore()
+    count = 1
+    pl.semaphore_signal(barrier, inc=1, device_id=partner, device_id_type=MESH)
+    for a in size:
+        for k in range(1, size[a]):
+            pl.semaphore_signal(barrier, inc=1, device_id=peer(a, k)[1], device_id_type=MESH)
+            count += 1
+    pl.semaphore_wait(barrier, count)
+
+    def remote(src, dst, send, recv, device):
+        copy = pltpu.make_async_remote_copy(
+            src_ref=src, dst_ref=dst, send_sem=send, recv_sem=recv, device_id=device, device_id_type=MESH
+        )
+        copy.start()
+        return copy
+
+    def rows_of(off, m):
+        return pl.ds(pl.multiple_of(off, 16), m)
+
+    length = w_ref.shape[0]
+    off = [q * (length // 2) for q in range(2)]
+    span = [length // 2] * 2
+
+    def start_reduce(q, ph):
+        a = plans[q][ph]
+        g = size[a]
+        m = span[q] // g
+        copies = []
+        for k in range(1, g):
+            p, dev = peer(a, k)
+            src = w_ref.at[rows_of(off[q] + p * m, m)] if ph == 0 else held[q][ph - 1].at[rows_of(p * m, m)]
+            copies.append(
+                remote(src, stage[q][ph].at[k - 1], w_send.at[q, ph, k - 1], w_recv.at[q, ph, k - 1], dev)
+            )
+        return copies
+
+    def finish_reduce(q, ph, copies):
+        a = plans[q][ph]
+        g = size[a]
+        m = span[q] // g
+        for c in copies:
+            c.wait()
+        mine = rows_of(off[q] + at[a] * m, m) if ph == 0 else rows_of(at[a] * m, m)
+        total = (w_ref[mine] if ph == 0 else held[q][ph - 1][mine]).astype(F32)
+        for k in range(g - 1):
+            total = total + stage[q][ph][k].astype(F32)
+        off[q] = off[q] + at[a] * m
+        span[q] = m
+        if ph < len(plans[q]) - 1:
+            held[q][ph][...] = total.astype(BF16)
+        else:
+            wout[core, rows_of(off[q], m)] = total.astype(BF16)
+
+    def start_sums(ph):
+        a = "xyz"[ph]
+        width = stride[a]
+        first = me // width * width
+        block = pl.ds(first, width)
+        return [
+            remote(sout.at[block], sout.at[block], s_send.at[ph, k - 1], s_recv.at[ph, k - 1], peer(a, k)[1])
+            for k in range(1, size[a])
+        ]
+
+    sout[me] = s_ref[...]
+    bout[core] = b_ref[...]
+    pending = [start_reduce(q, 0) for q in range(2)]
+    sums = start_sums(0)
+    basis_copy = remote(b_ref, bout.at[core], c_send.at[2], c_recv.at[2], partner)
+    for ph in range(3):
+        for c in sums:
+            c.wait()
+        if ph < 2:
+            sums = start_sums(ph + 1)
+        for q in range(2):
+            finish_reduce(q, ph, pending[q])
+            if ph < 2:
+                pending[q] = start_reduce(q, ph + 1)
+
+    def start_gather(q, ph):
+        a = plans[q][ph]
+        block = wout.at[core, rows_of(off[q], span[q])]
+        return [
+            remote(block, block, w_send.at[q, 3 + ph, k - 1], w_recv.at[q, 3 + ph, k - 1], peer(a, k)[1])
+            for k in range(1, size[a])
+        ]
+
+    pending = [start_gather(q, 2) for q in range(2)]
+    across = []
+    for ph in (2, 1, 0):
+        for q in range(2):
+            a = plans[q][ph]
+            for c in pending[q]:
+                c.wait()
+            off[q] = off[q] - at[a] * span[q]
+            span[q] = span[q] * size[a]
+            if ph > 0:
+                pending[q] = start_gather(q, ph - 1)
+            if ph == 1:
+                early = rows_of(off[q], span[q])
+                block = wout.at[core, early]
+                across.append(remote(block, block, c_send.at[q], c_recv.at[q], partner))
+    for q in range(2):
+        a = plans[q][0]
+        part = span[q] // size[a]
+        for k in range(1, size[a]):
+            p = peer(a, k)[0]
+            block = wout.at[core, rows_of(off[q] + p * part, part)]
+            across.append(remote(block, block, c_send.at[2 + q * 3 + k], c_recv.at[2 + q * 3 + k], partner))
+    for c in across:
+        c.wait()
+    basis_copy.wait()
+
+
+def reduce(r, w, s, b):
+    length = w.shape[0]
+    nz, ny, nx = factors(r)
+    stages, helds = [], []
+    for sizes in ((nx, ny, nz), (ny, nx, nz)):
+        m = length // 2
+        for ph, g in enumerate(sizes):
+            m //= g
+            stages.append(pltpu.VMEM((max(g - 1, 1), m, LANES), BF16))
+            if ph < 2:
+                helds.append(pltpu.VMEM((m, LANES), BF16))
+    widest = max(nx, ny, nz) - 1
+    vm = pl.BlockSpec(memory_space=pltpu.VMEM)
+    dma = pltpu.SemaphoreType.DMA
+    return pl.pallas_call(
+        functools.partial(reduce_kernel, r),
+        in_specs=[vm] * 3,
+        out_specs=[vm] * 3,
+        out_shape=[
+            jax.ShapeDtypeStruct((2,) + w.shape, BF16),
+            jax.ShapeDtypeStruct((r,) + s.shape, F32),
+            jax.ShapeDtypeStruct((2,) + b.shape, BF16),
+        ],
+        scratch_shapes=stages + helds + [dma((2, 6, widest)), dma((2, 6, widest)), dma((3, widest)), dma((3, widest)), dma((9,)), dma((9,))],
+        compiler_params=pltpu.CompilerParams(collective_id=0, has_side_effects=True),
+    )(w, s, b)
+
+
 def shards(embeddings, start_basis):
     n, d = embeddings.shape
     total = n * lax.axis_size("rows")
     w, s = scatter(embeddings)
-    w = lax.psum(w, "rows")
-    w = lax.all_gather(w, "cols", axis=0)
-    s = lax.all_gather(s[0], "rows", axis=0)
-    b = lax.all_gather(start_basis.astype(BF16), "cols", axis=1, tiled=True)
+    shape = w.shape
+    w, s, b = reduce(lax.axis_size("rows"), w.reshape(-1, LANES), s, start_basis.astype(BF16))
+    w = w.reshape((2,) + shape)
     basis = iterate(n, total, w, s, b)
     return project(total, embeddings, s, basis, start_basis.shape[1])
 

time: 308 us -> 190 us (0.62)
  waiting for transfers between devices: 120 us -> 0 us
  Pallas kernels: 129 us -> 186 us
  blocking collectives: 41.9 us -> 0 us
  between operations: 14.1 us -> 0.64 us
    psum x1 -> x0, waiting for transfers between devices: 120 us -> none  [shards(): w = lax.psum(w, 'rows')]
    pallas_call x0 -> x1, Pallas kernels: none -> 56.8 us  [reduce(): pl.pallas_call(functools.partial(reduce_kernel, r), in_specs=[vm] * 3, ou...]
    all_gather x2 -> x0, blocking collectives: 41.9 us -> none  [the longest x1 39.4 us: shards(): s = lax.all_gather(s[0], 'rows', axis=0)]
  transfers between devices with their start and end apart: 2 -> 0, of which waited for: 1 -> 0; matrix products, arithmetic and copies ran while one was open for 0% -> 0% of each run, Pallas kernels for 0% -> 0%
where the time goes in v2:
time: 190 us; the launch traced here: 189 us
  Pallas kernels  186 us (98%)
  other arithmetic  1.92 us (1%)
    pallas_call x1, Pallas kernels, iterate(): pl.pallas_call(functools.partial(iterate_kernel, n, total), in_specs=[vm]...  106 us
    pallas_call x1, Pallas kernels, reduce(): pl.pallas_call(functools.partial(reduce_kernel, r), in_specs=[vm] * 3, ou...  56.8 us
    pallas_call x1, Pallas kernels, scatter(): pl.pallas_call(functools.partial(scatter_kernel, n), grid=(n // rows,), i...  13.7 us
    pallas_call x1, Pallas kernels, project(): pl.pallas_call(functools.partial(project_kernel, total), grid=(n // rows,...  10.1 us

profile of v2, /device:TPU:0, one launch (start us, length us, event | category | flops | bytes accessed | tf_op | source)
XLA Modules:
  0.0 188.9 jit_solution(6914334530442400137)
XLA Ops:
  0.6 1.9 %convert_element_type.3.b_ref = bf16[1536,128]{1,0:T(8,128)(2,1)} convert(f32[1536,128]{1,0:T(8,128)} %param.3) | non-fusion elementwise | flops 196608 | bytes 1179648 | tf_op jit(solution)/shard_map/convert_element_type | solution.py:365
  2.5 13.7 %shard_map.41 = (bf16[3,4,512,128]{3,2,1,0:T(8,128)(2,1)}, f32[1,1536]{1,0:T(1,128)}) custom-call(bf16[3072,1536]{1,0:T(8,128)(2,1)} %e_ref.3), custom_call_target="tpu_custom_call" | custom-call | tf_op jit(solution)/shard_map/pallas_call | solution.py:66
  16.2 56.8 %shard_map.42 = (bf16[2,6144,128]{2,1,0:T(8,128)(2,1)}, f32[16,1,1536]{2,1,0:T(1,128)}, bf16[2,1536,128]{2,1,0:T(8,128)(2,1)}) custom-call(bf16[6144,128]{1,0:T(8,128)(2,1)} %bitcast.3, f32[1,1536]{1,0:T(1,128)} %get-tuple-element.8.s_ref, bf16[1536,128]{1,0:T(8,128)(2,1)} %convert_element_type.3.b_ref), custom_call_target="tpu_custom_call" | custom-call | tf_op jit(solution)/shard_map/pallas_call | solution.py:346
  73.0 105.8 %shard_map.43.b_ref = f32[1536,256]{1,0:T(8,128)} custom-call(bf16[2,3,4,512,128]{4,3,2,1,0:T(8,128)(2,1)} %bitcast.2, f32[16,1,1536]{2,1,0:T(1,128)} %get-tuple-element.9.s_ref, bf16[2,1536,128]{2,1,0:T(8,128)(2,1)} %get-tuple-element.11.b_ref), custom_call_target="tpu_custom_call" | custom-call | tf_op jit(solution)/shard_map/pallas_call | solution.py:142
  178.8 10.1 %shard_map.44 = (bf16[3072,128]{1,0:T(8,128)(2,1)}, f32[1536,128]{1,0:T(8,128)}) custom-call(bf16[3072,1536]{1,0:T(8,128)(2,1)} %e_ref.3, f32[16,1,1536]{2,1,0:T(1,128)} %get-tuple-element.9.s_ref, f32[1536,256]{1,0:T(8,128)} %shard_map.43.b_ref), custom_call_target="tpu_custom_call" | custom-call | tf_op jit(solution)/shard_map/pallas_call | solution.py:178

commit v3 on v2

--- a/solution.py
+++ b/solution.py
@@ -79,35 +79,76 @@
     )(e)
 
 
+def split(v):
+    hi = v.astype(BF16)
+    return hi, (v - hi.astype(F32)).astype(BF16)
+
+
+def pivot_inverse(a):
+    m = len(a)
+    a = [list(row) for row in a]
+    t = [[None] * m for _ in range(m)]
+    inv = []
+    for j in range(m):
+        r = 1.0 / a[j][j]
+        inv.append(r)
+        for i in range(j + 1, m):
+            f = a[i][j] * r
+            for c in range(j + 1, i + 1):
+                a[i][c] = a[i][c] - f * a[c][j]
+            for c in range(j):
+                t[i][c] = t[i][c] - f * t[j][c]
+            t[i][j] = -f
+    return t, inv
+
+
 def inverse_factor(a_ref, k, b):
-    sub = lax.broadcasted_iota(jnp.int32, (8, 2 * b), 0)
+    w = 2 * b
+    sub = lax.broadcasted_iota(jnp.int32, (8, w), 0)
     eye = (lax.broadcasted_iota(jnp.int32, (b, b), 0) == lax.broadcasted_iota(jnp.int32, (b, b), 1)).astype(F32)
     for blk in range(k // b):
         lo, hi = blk * b, (blk + 1) * b
         aug = jnp.concatenate([a_ref[lo:hi, lo:hi], eye], axis=1)
         tiles = [aug[8 * t:8 * t + 8] for t in range(b // 8)]
-        for j in range(b):
-            tj, r = j // 8, j % 8
-            cols = {t: jnp.broadcast_to(tiles[t][:, j:j + 1], (8, 2 * b)) for t in range(tj, b // 8)}
-            row = tiles[tj][r:r + 1] * (1.0 / cols[tj][r:r + 1])
-            for t in range(tj, b // 8):
-                f = cols[t]
-                if t == tj:
-                    if r == 7:
-                        continue
-                    f = jnp.where(sub > r, f, 0.0)
-                tiles[t] = tiles[t] - f * row
-        aug = jnp.concatenate(tiles, axis=0)
-        diag = jnp.sum(aug[:, :b] * eye, axis=1, keepdims=True)
-        scale = lax.rsqrt(diag)
-        scale = scale * (1.5 - 0.5 * diag * scale * scale)
-        strip = dot(aug[:, b:] * scale, a_ref[lo:hi, :], 1, 0, HI)
+        for p in range(b // 8):
+            cols = {
+                t: [jnp.broadcast_to(tiles[t][:, 8 * p + c:8 * p + c + 1], (8, w)) for c in range(8)]
+                for t in range(p, b // 8)
+            }
+            block = [[jnp.broadcast_to(cols[p][j][i:i + 1], (8, w)) for j in range(i + 1)] for i in range(8)]
+            t8, inv = pivot_inverse(block)
+            rows = [jnp.broadcast_to(tiles[p][c:c + 1], (8, w)) for c in range(8)]
+            low = []
+            for i in range(8):
+                v = rows[i]
+                for c in range(i):
+                    v = v + t8[i][c] * rows[c]
+                low.append(v)
+            scaled = [low[i] * inv[i] for i in range(8)]
+            if p + 1 < b // 8:
+                solved = []
+                for c in range(8):
+                    v = scaled[c]
+                    for i in range(c + 1, 8):
+                        v = v + t8[i][c] * scaled[i]
+                    solved.append(v)
+                for t in range(p + 1, b // 8):
+                    u = [cols[t][c] * solved[c] for c in range(8)]
+                    tiles[t] = tiles[t] - (((u[0] + u[1]) + (u[2] + u[3])) + ((u[4] + u[5]) + (u[6] + u[7])))
+            v, d = low[0], inv[0]
+            for i in range(1, 8):
+                v = jnp.where(sub == i, low[i], v)
+                d = jnp.where(sub == i, inv[i], d)
+            root = lax.rsqrt(d)
+            root = root * (1.5 - 0.5 * d * root * root)
+            tiles[p] = v * (d * root)
+        strip = dot(jnp.concatenate(tiles, axis=0)[:, b:], a_ref[lo:hi, :], 1, 0, HI)
         a_ref[lo:hi, :] = strip
         if hi < k:
             a_ref[hi:, :] -= dot(strip[:, hi:k], strip, 0, 0, HI)
 
 
-def iterate_kernel(n, total, w_ref, s_ref, b_ref, out_ref, w, basis, mean, a):
+def iterate_kernel(n, total, w_ref, s_ref, b_ref, out_ref, w, basis, mean, mean_t, a):
     d, k = out_ref.shape
     t = d // PARTS
     for c, pairs in enumerate((((0, 0), (0, 1), (0, 2)), ((1, 1), (1, 2), (2, 2)))):
@@ -117,21 +158,28 @@
             if i != j:
                 w[j * t:(j + 1) * t, i * t:(i + 1) * t] = v.T
     s = s_ref[:, 0, :]
-    mean[...] = s * (1.0 / n) - jnp.sum(s, axis=0, keepdims=True) * (1.0 / total)
+    r = s.shape[0]
+    m = s * (1.0 / n) - jnp.sum(s, axis=0, keepdims=True) * (1.0 / total)
+    mh, ml = split(m)
+    mean[:r] = mh
+    mean[r:] = ml
+    mean_t[...] = jnp.concatenate([mh.astype(F32), ml.astype(F32), mh.astype(F32)], axis=0).T.astype(BF16)
     basis[...] = jnp.concatenate([b_ref[0], b_ref[1]], axis=1)
 
     @pl.loop(0, ITERS)
     def _(_):
         bf = basis[...]
-        m = mean[...]
-        inner = dot(m, bf.astype(F32), 1, 0, HI) * float(n)
-        products = dot(w[...], bf, 1, 0) + dot(m, inner, 0, 0, HI)
-        a[:, :k] = dot(products, products, 0, 0, HI)
+        inner = dot(mean[...], bf, 1, 0)
+        ih, il = split((inner[:r] + inner[r:]) * float(n))
+        ph, plo = split(dot(w[...], bf, 1, 0) + dot(mean_t[...], jnp.concatenate([ih, ih, il], axis=0), 1, 0))
+        cross = dot(plo, ph, 0, 0)
+        a[:, :k] = dot(ph, ph, 0, 0) + (dot(plo, plo, 0, 0) + (cross + cross.T))
         a[:, k:] = (
             lax.broadcasted_iota(jnp.int32, (k, k), 0) == lax.broadcasted_iota(jnp.int32, (k, k), 1)
         ).astype(F32)
         inverse_factor(a, k, 64)
-        new = dot(products, a[:, k:], 1, 1, HI)
+        lh, ll = split(a[:, k:])
+        new = dot(ph, lh, 1, 1) + (dot(ph, ll, 1, 1) + dot(plo, lh, 1, 1))
         out_ref[...] = new
         basis[...] = new.astype(BF16)
 
@@ -147,7 +195,8 @@
         scratch_shapes=[
             pltpu.VMEM((d, d), BF16),
             pltpu.VMEM((d, k), BF16),
-            pltpu.VMEM((s.shape[0], d), F32),
+            pltpu.VMEM((2 * s.shape[0], d), BF16),
+            pltpu.VMEM((d, 3 * s.shape[0]), BF16),
             pltpu.VMEM((k, 2 * k), F32),
         ],
     )(w, s, b)

time: 190 us -> 138 us (0.73)
  Pallas kernels: 186 us -> 134 us
    pallas_call x1, Pallas kernels: 106 us -> 53.5 us  [iterate(): pl.pallas_call(functools.partial(iterate_kernel, n, total), in_specs=[vm]...]
where the time goes in v3:
time: 138 us; the launch traced here: 137 us
  Pallas kernels  134 us (97%)
  other arithmetic  1.92 us (1%)
    pallas_call x1, Pallas kernels, reduce(): pl.pallas_call(functools.partial(reduce_kernel, r), in_specs=[vm] * 3, ou...  56.8 us
    pallas_call x1, Pallas kernels, iterate(): pl.pallas_call(functools.partial(iterate_kernel, n, total), in_specs=[vm]...  53.5 us
    pallas_call x1, Pallas kernels, scatter(): pl.pallas_call(functools.partial(scatter_kernel, n), grid=(n // rows,), i...  13.7 us
    pallas_call x1, Pallas kernels, project(): pl.pallas_call(functools.partial(project_kernel, total), grid=(n // rows,...  10.1 us

profile of v3, /device:TPU:0, one launch (start us, length us, event | category | flops | bytes accessed | tf_op | source)
XLA Modules:
  0.0 136.6 jit_solution(14181473452224516974)
XLA Ops:
  0.6 1.9 %convert_element_type.3.b_ref = bf16[1536,128]{1,0:T(8,128)(2,1)} convert(f32[1536,128]{1,0:T(8,128)} %param.3) | non-fusion elementwise | flops 196608 | bytes 1179648 | tf_op jit(solution)/shard_map/convert_element_type | solution.py:414
  2.5 13.7 %shard_map.41 = (bf16[3,4,512,128]{3,2,1,0:T(8,128)(2,1)}, f32[1,1536]{1,0:T(1,128)}) custom-call(bf16[3072,1536]{1,0:T(8,128)(2,1)} %e_ref.3), custom_call_target="tpu_custom_call" | custom-call | tf_op jit(solution)/shard_map/pallas_call | solution.py:66
  16.2 56.8 %shard_map.42 = (bf16[2,6144,128]{2,1,0:T(8,128)(2,1)}, f32[16,1,1536]{2,1,0:T(1,128)}, bf16[2,1536,128]{2,1,0:T(8,128)(2,1)}) custom-call(bf16[6144,128]{1,0:T(8,128)(2,1)} %bitcast.3, f32[1,1536]{1,0:T(1,128)} %get-tuple-element.8.s_ref, bf16[1536,128]{1,0:T(8,128)(2,1)} %convert_element_type.3.b_ref), custom_call_target="tpu_custom_call" | custom-call | tf_op jit(solution)/shard_map/pallas_call | solution.py:395
  73.0 53.5 %shard_map.43.b_ref = f32[1536,256]{1,0:T(8,128)} custom-call(bf16[2,3,4,512,128]{4,3,2,1,0:T(8,128)(2,1)} %bitcast.2, f32[16,1,1536]{2,1,0:T(1,128)} %get-tuple-element.9.s_ref, bf16[2,1536,128]{2,1,0:T(8,128)(2,1)} %get-tuple-element.11.b_ref), custom_call_target="tpu_custom_call" | custom-call | tf_op jit(solution)/shard_map/pallas_call | solution.py:190
  126.5 10.1 %shard_map.44 = (bf16[3072,128]{1,0:T(8,128)(2,1)}, f32[1536,128]{1,0:T(8,128)}) custom-call(bf16[3072,1536]{1,0:T(8,128)(2,1)} %e_ref.3, f32[16,1,1536]{2,1,0:T(1,128)} %get-tuple-element.9.s_ref, f32[1536,256]{1,0:T(8,128)} %shard_map.43.b_ref), custom_call_target="tpu_custom_call" | custom-call | tf_op jit(solution)/shard_map/pallas_call | solution.py:227

commit v4 on v3

--- a/solution.py
+++ b/solution.py
@@ -11,6 +11,7 @@
 PARTS = 3
 LANES = 128
 MESH = pl.DeviceIdType.MESH
+STREAMS = 2 * PARTS
 HI = lax.Precision.HIGHEST
 F32 = jnp.float32
 BF16 = jnp.bfloat16
@@ -248,7 +249,7 @@
 
 def reduce_kernel(r, w_ref, s_ref, b_ref, wout, sout, bout, *scratch):
     nz, ny, nx = factors(r)
-    plans = (("x", "y", "z"), ("y", "x", "z"))
+    plans = (("x", "y", "z"), ("y", "x", "z")) * (STREAMS // 2)
     size = {"x": nx, "y": ny, "z": nz}
     stride = {"x": 1, "y": nx, "z": nx * ny}
     scratch = list(scratch)
@@ -285,8 +286,8 @@
         return pl.ds(pl.multiple_of(off, 16), m)
 
     length = w_ref.shape[0]
-    off = [q * (length // 2) for q in range(2)]
-    span = [length // 2] * 2
+    off = [q * (length // STREAMS) for q in range(STREAMS)]
+    span = [length // STREAMS] * STREAMS
 
     def start_reduce(q, ph):
         a = plans[q][ph]
@@ -330,15 +331,15 @@
 
     sout[me] = s_ref[...]
     bout[core] = b_ref[...]
-    pending = [start_reduce(q, 0) for q in range(2)]
+    pending = [start_reduce(q, 0) for q in range(STREAMS)]
     sums = start_sums(0)
-    basis_copy = remote(b_ref, bout.at[core], c_send.at[2], c_recv.at[2], partner)
+    basis_copy = remote(b_ref, bout.at[core], c_send.at[STREAMS], c_recv.at[STREAMS], partner)
     for ph in range(3):
         for c in sums:
             c.wait()
         if ph < 2:
             sums = start_sums(ph + 1)
-        for q in range(2):
+        for q in range(STREAMS):
             finish_reduce(q, ph, pending[q])
             if ph < 2:
                 pending[q] = start_reduce(q, ph + 1)
@@ -351,10 +352,10 @@
             for k in range(1, size[a])
         ]
 
-    pending = [start_gather(q, 2) for q in range(2)]
+    pending = [start_gather(q, 2) for q in range(STREAMS)]
     across = []
     for ph in (2, 1, 0):
-        for q in range(2):
+        for q in range(STREAMS):
             a = plans[q][ph]
             for c in pending[q]:
                 c.wait()
@@ -366,13 +367,13 @@
                 early = rows_of(off[q], span[q])
                 block = wout.at[core, early]
                 across.append(remote(block, block, c_send.at[q], c_recv.at[q], partner))
-    for q in range(2):
-        a = plans[q][0]
-        part = span[q] // size[a]
-        for k in range(1, size[a]):
-            p = peer(a, k)[0]
-            block = wout.at[core, rows_of(off[q] + p * part, part)]
-            across.append(remote(block, block, c_send.at[2 + q * 3 + k], c_recv.at[2 + q * 3 + k], partner))
+            if ph == 0:
+                part = span[q] // size[a]
+                for k in range(1, size[a]):
+                    p = peer(a, k)[0]
+                    block = wout.at[core, rows_of(off[q] + p * part, part)]
+                    sem = STREAMS + q * (size[a] - 1) + k
+                    across.append(remote(block, block, c_send.at[sem], c_recv.at[sem], partner))
     for c in across:
         c.wait()
     basis_copy.wait()
@@ -382,14 +383,15 @@
     length = w.shape[0]
     nz, ny, nx = factors(r)
     stages, helds = [], []
-    for sizes in ((nx, ny, nz), (ny, nx, nz)):
-        m = length // 2
+    for sizes in ((nx, ny, nz), (ny, nx, nz)) * (STREAMS // 2):
+        m = length // STREAMS
         for ph, g in enumerate(sizes):
             m //= g
             stages.append(pltpu.VMEM((max(g - 1, 1), m, LANES), BF16))
             if ph < 2:
                 helds.append(pltpu.VMEM((m, LANES), BF16))
     widest = max(nx, ny, nz) - 1
+    sems = ((STREAMS, 6, widest), (3, widest), (1 + STREAMS * (1 + widest),))
     vm = pl.BlockSpec(memory_space=pltpu.VMEM)
     dma = pltpu.SemaphoreType.DMA
     return pl.pallas_call(
@@ -401,7 +403,7 @@
             jax.ShapeDtypeStruct((r,) + s.shape, F32),
             jax.ShapeDtypeStruct((2,) + b.shape, BF16),
         ],
-        scratch_shapes=stages + helds + [dma((2, 6, widest)), dma((2, 6, widest)), dma((3, widest)), dma((3, widest)), dma((9,)), dma((9,))],
+        scratch_shapes=stages + helds + [dma(shape) for shape in sems for _ in range(2)],
         compiler_params=pltpu.CompilerParams(collective_id=0, has_side_effects=True),
     )(w, s, b)
 

time: 138 us -> 135 us (0.978)
  Pallas kernels: 134 us -> 132 us
    pallas_call x1, Pallas kernels: 56.8 us -> 54.6 us  [reduce(): pl.pallas_call(functools.partial(reduce_kernel, r), in_specs=[vm] * 3, ou...]
where the time goes in v4:
time: 135 us; the launch traced here: 134 us
  Pallas kernels  132 us (98%)
  other arithmetic  1.92 us (1%)
    pallas_call x1, Pallas kernels, reduce(): pl.pallas_call(functools.partial(reduce_kernel, r), in_specs=[vm] * 3, ou...  54.6 us
    pallas_call x1, Pallas kernels, iterate(): pl.pallas_call(functools.partial(iterate_kernel, n, total), in_specs=[vm]...  53.5 us
    pallas_call x1, Pallas kernels, scatter(): pl.pallas_call(functools.partial(scatter_kernel, n), grid=(n // rows,), i...  13.7 us
    pallas_call x1, Pallas kernels, project(): pl.pallas_call(functools.partial(project_kernel, total), grid=(n // rows,...  10.1 us

profile of v4, /device:TPU:0, one launch (start us, length us, event | category | flops | bytes accessed | tf_op | source)
XLA Modules:
  0.0 134.4 jit_solution(10768263950263218029)
XLA Ops:
  0.6 1.9 %convert_element_type.3.b_ref = bf16[1536,128]{1,0:T(8,128)(2,1)} convert(f32[1536,128]{1,0:T(8,128)} %param.3) | non-fusion elementwise | flops 196608 | bytes 1179648 | tf_op jit(solution)/shard_map/convert_element_type | solution.py:416
  2.5 13.7 %shard_map.41 = (bf16[3,4,512,128]{3,2,1,0:T(8,128)(2,1)}, f32[1,1536]{1,0:T(1,128)}) custom-call(bf16[3072,1536]{1,0:T(8,128)(2,1)} %e_ref.3), custom_call_target="tpu_custom_call" | custom-call | tf_op jit(solution)/shard_map/pallas_call | solution.py:67
  16.2 54.6 %shard_map.42 = (bf16[2,6144,128]{2,1,0:T(8,128)(2,1)}, f32[16,1,1536]{2,1,0:T(1,128)}, bf16[2,1536,128]{2,1,0:T(8,128)(2,1)}) custom-call(bf16[6144,128]{1,0:T(8,128)(2,1)} %bitcast.3, f32[1,1536]{1,0:T(1,128)} %get-tuple-element.8.s_ref, bf16[1536,128]{1,0:T(8,128)(2,1)} %convert_element_type.3.b_ref), custom_call_target="tpu_custom_call" | custom-call | tf_op jit(solution)/shard_map/pallas_call | solution.py:397
  70.8 53.5 %shard_map.43.b_ref = f32[1536,256]{1,0:T(8,128)} custom-call(bf16[2,3,4,512,128]{4,3,2,1,0:T(8,128)(2,1)} %bitcast.2, f32[16,1,1536]{2,1,0:T(1,128)} %get-tuple-element.9.s_ref, bf16[2,1536,128]{2,1,0:T(8,128)(2,1)} %get-tuple-element.11.b_ref), custom_call_target="tpu_custom_call" | custom-call | tf_op jit(solution)/shard_map/pallas_call | solution.py:191
  124.3 10.1 %shard_map.44 = (bf16[3072,128]{1,0:T(8,128)(2,1)}, f32[1536,128]{1,0:T(8,128)}) custom-call(bf16[3072,1536]{1,0:T(8,128)(2,1)} %e_ref.3, f32[16,1,1536]{2,1,0:T(1,128)} %get-tuple-element.9.s_ref, f32[1536,256]{1,0:T(8,128)} %shard_map.43.b_ref), custom_call_target="tpu_custom_call" | custom-call | tf_op jit(solution)/shard_map/pallas_call | solution.py:228

commit v5 on v4

--- a/solution.py
+++ b/solution.py
@@ -12,6 +12,7 @@
 LANES = 128
 MESH = pl.DeviceIdType.MESH
 STREAMS = 2 * PARTS
+TILES = 4
 HI = lax.Precision.HIGHEST
 F32 = jnp.float32
 BF16 = jnp.bfloat16
@@ -21,63 +22,7 @@
     return lax.dot_general(a, b, (((ca,), (cb,)), ((), ())), precision=precision, preferred_element_type=F32)
 
 
-def scatter_kernel(n, e_ref, w_ref, s_ref, acc, sums):
-    step = pl.program_id(0)
-    core = lax.axis_index("cols")
-    t = acc.shape[1]
-
-    @pl.when(step == 0)
-    def _():
-        acc[...] = jnp.zeros_like(acc)
-        sums[...] = jnp.zeros_like(sums)
-
-    e = e_ref[...]
-    sums[...] += dot(jnp.ones((8, e.shape[0]), BF16), e, 1, 0)
-
-    def block(slot, i, j):
-        acc[slot] += dot(e[:, i * t:(i + 1) * t], e[:, j * t:(j + 1) * t], 0, 0)
-
-    def finish(slot, i, j):
-        si = sums[:, i * t:(i + 1) * t] * (1.0 / (8 * n))
-        sj = sums[:, j * t:(j + 1) * t]
-        v = (acc[slot] - dot(si, sj, 0, 0, HI)).astype(w_ref.dtype)
-        for c in range(t // LANES):
-            w_ref[slot, c] = v[:, c * LANES:(c + 1) * LANES]
-
-    last = step == pl.num_programs(0) - 1
-    for c, pairs in enumerate((((0, 0), (0, 1), (0, 2)), ((1, 1), (1, 2), (2, 2)))):
-        @pl.when(core == c)
-        def _(pairs=pairs):
-            for slot, (i, j) in enumerate(pairs):
-                block(slot, i, j)
-
-            @pl.when(last)
-            def _():
-                for slot, (i, j) in enumerate(pairs):
-                    finish(slot, i, j)
-
-    @pl.when(last)
-    def _():
-        s_ref[...] = sums[0:1, :]
-
-
-def scatter(e, rows=512):
-    n, d = e.shape
-    t = d // PARTS
-    return pl.pallas_call(
-        functools.partial(scatter_kernel, n),
-        grid=(n // rows,),
-        in_specs=[pl.BlockSpec((rows, d), lambda i: (i, 0))],
-        out_specs=[
-            pl.BlockSpec((PARTS, t // LANES, t, LANES), lambda i: (0, 0, 0, 0)),
-            pl.BlockSpec((1, d), lambda i: (0, 0)),
-        ],
-        out_shape=[
-            jax.ShapeDtypeStruct((PARTS, t // LANES, t, LANES), BF16),
-            jax.ShapeDtypeStruct((1, d), F32),
-        ],
-        scratch_shapes=[pltpu.VMEM((PARTS, t, t), F32), pltpu.VMEM((8, d), F32)],
-    )(e)
+BLOCKS = (((0, 0), (0, 1), (0, 2)), ((1, 1), (1, 2), (2, 2)))
 
 
 def split(v):
@@ -152,7 +97,7 @@
 def iterate_kernel(n, total, w_ref, s_ref, b_ref, out_ref, w, basis, mean, mean_t, a):
     d, k = out_ref.shape
     t = d // PARTS
-    for c, pairs in enumerate((((0, 0), (0, 1), (0, 2)), ((1, 1), (1, 2), (2, 2)))):
+    for c, pairs in enumerate(BLOCKS):
         for slot, (i, j) in enumerate(pairs):
             v = jnp.concatenate([w_ref[c, slot, l] for l in range(t // LANES)], axis=1)
             w[i * t:(i + 1) * t, j * t:(j + 1) * t] = v
@@ -247,7 +192,7 @@
     return z, r // z // x, x
 
 
-def reduce_kernel(r, w_ref, s_ref, b_ref, wout, sout, bout, *scratch):
+def reduce_kernel(r, e_hbm, b_ref, wout, sout, bout, e, acc, ssum, w_ref, e_sem, *scratch):
     nz, ny, nx = factors(r)
     plans = (("x", "y", "z"), ("y", "x", "z")) * (STREAMS // 2)
     size = {"x": nx, "y": ny, "z": nz}
@@ -259,6 +204,16 @@
 
     me = lax.axis_index("rows")
     core = lax.axis_index("cols")
+    n, d = e.shape
+    t = d // PARTS
+    tile = n // TILES
+
+    def tile_copy(i):
+        at_rows = pl.ds(pl.multiple_of(i * tile, tile), tile)
+        return pltpu.make_async_copy(e_hbm.at[at_rows], e.at[at_rows], e_sem.at[i])
+
+    for i in range(TILES):
+        tile_copy(i).start()
     at = {a: lax.rem(me // stride[a], size[a]) for a in size}
     partner = {"cols": 1 - core}
 
@@ -329,17 +284,49 @@
             for k in range(1, size[a])
         ]
 
-    sout[me] = s_ref[...]
     bout[core] = b_ref[...]
-    pending = [start_reduce(q, 0) for q in range(STREAMS)]
-    sums = start_sums(0)
     basis_copy = remote(b_ref, bout.at[core], c_send.at[STREAMS], c_recv.at[STREAMS], partner)
+    ssum[...] = jnp.zeros_like(ssum)
+    pending = []
+    for slot in range(PARTS):
+        acc[...] = jnp.zeros_like(acc)
+        for c in range(2):
+            @pl.when(core == c)
+            def _(slot=slot, c=c):
+                i, j = BLOCKS[c][slot]
+
+                @pl.loop(0, TILES)
+                def _(step):
+                    if slot == 0:
+                        tile_copy(step).wait()
+                    part = pl.ds(pl.multiple_of(step * tile, tile), tile)
+                    if slot == 0:
+                        ssum[...] += dot(jnp.ones((8, tile), BF16), e[part, :], 1, 0)
+                    acc[...] += dot(e[part, i * t:(i + 1) * t], e[part, j * t:(j + 1) * t], 0, 0)
+
+                si = ssum[:, i * t:(i + 1) * t] * (1.0 / (8 * n))
+                v = (acc[...] - dot(si, ssum[:, j * t:(j + 1) * t], 0, 0, HI)).astype(BF16)
+                for l in range(t // LANES):
+                    first = (slot * (t // LANES) + l) * t
+                    w_ref[first:first + t, :] = v[:, l * LANES:(l + 1) * LANES]
+
+        if slot == 0:
+            sout[me] = ssum[0:1, :]
+        pending += [start_reduce(q, 0) for q in (2 * slot, 2 * slot + 1)]
+        if slot == 0:
+            sums = start_sums(0)
+        else:
+            for q in (2 * slot - 2, 2 * slot - 1):
+                finish_reduce(q, 0, pending[q])
+                pending[q] = start_reduce(q, 1)
     for ph in range(3):
         for c in sums:
             c.wait()
         if ph < 2:
             sums = start_sums(ph + 1)
         for q in range(STREAMS):
+            if ph == 0 and q < STREAMS - 2:
+                continue
             finish_reduce(q, ph, pending[q])
             if ph < 2:
                 pending[q] = start_reduce(q, ph + 1)
@@ -379,8 +366,10 @@
     basis_copy.wait()
 
 
-def reduce(r, w, s, b):
-    length = w.shape[0]
+def reduce(r, e, b):
+    n, d = e.shape
+    t = d // PARTS
+    length = PARTS * t * t // LANES
     nz, ny, nx = factors(r)
     stages, helds = [], []
     for sizes in ((nx, ny, nz), (ny, nx, nz)) * (STREAMS // 2):
@@ -396,25 +385,31 @@
     dma = pltpu.SemaphoreType.DMA
     return pl.pallas_call(
         functools.partial(reduce_kernel, r),
-        in_specs=[vm] * 3,
+        in_specs=[pl.BlockSpec(memory_space=pl.ANY), vm],
         out_specs=[vm] * 3,
         out_shape=[
-            jax.ShapeDtypeStruct((2,) + w.shape, BF16),
-            jax.ShapeDtypeStruct((r,) + s.shape, F32),
+            jax.ShapeDtypeStruct((2, length, LANES), BF16),
+            jax.ShapeDtypeStruct((r, 1, d), F32),
             jax.ShapeDtypeStruct((2,) + b.shape, BF16),
         ],
-        scratch_shapes=stages + helds + [dma(shape) for shape in sems for _ in range(2)],
+        scratch_shapes=[
+            pltpu.VMEM((n, d), BF16),
+            pltpu.VMEM((t, t), F32),
+            pltpu.VMEM((8, d), F32),
+            pltpu.VMEM((length, LANES), BF16),
+            dma((TILES,)),
+        ]
+        + stages + helds + [dma(shape) for shape in sems for _ in range(2)],
         compiler_params=pltpu.CompilerParams(collective_id=0, has_side_effects=True),
-    )(w, s, b)
+    )(e, b)
 
 
 def shards(embeddings, start_basis):
     n, d = embeddings.shape
     total = n * lax.axis_size("rows")
-    w, s = scatter(embeddings)
-    shape = w.shape
-    w, s, b = reduce(lax.axis_size("rows"), w.reshape(-1, LANES), s, start_basis.astype(BF16))
-    w = w.reshape((2,) + shape)
+    t = d // PARTS
+    w, s, b = reduce(lax.axis_size("rows"), embeddings, start_basis.astype(BF16))
+    w = w.reshape(2, PARTS, t // LANES, t, LANES)
     basis = iterate(n, total, w, s, b)
     return project(total, embeddings, s, basis, start_basis.shape[1])
 

time: 135 us -> 127 us (0.941)
  Pallas kernels: 132 us -> 124 us
    pallas_call x2 -> x1, Pallas kernels: 68.2 us -> 60.9 us  [reduce(): pl.pallas_call(functools.partial(reduce_kernel, r), in_specs=[pl.BlockSpe...]
where the time goes in v5:
time: 127 us
  Pallas kernels  124 us (98%)
  other arithmetic  1.92 us (2%)
    pallas_call x1, Pallas kernels, reduce(): pl.pallas_call(functools.partial(reduce_kernel, r), in_specs=[pl.BlockSpe...  60.9 us
    pallas_call x1, Pallas kernels, iterate(): pl.pallas_call(functools.partial(iterate_kernel, n, total), in_specs=[vm]...  53.5 us
    pallas_call x1, Pallas kernels, project(): pl.pallas_call(functools.partial(project_kernel, total), grid=(n // rows,...  10.1 us

profile of v5, /device:TPU:0, one launch (start us, length us, event | category | flops | bytes accessed | tf_op | source)
XLA Modules:
  0.0 127.1 jit_solution(8902952984707282259)
XLA Ops:
  0.6 1.9 %convert_element_type.3.b_ref = bf16[1536,128]{1,0:T(8,128)(2,1)} convert(f32[1536,128]{1,0:T(8,128)} %param.3) | non-fusion elementwise | flops 196608 | bytes 1179648 | tf_op jit(solution)/shard_map/convert_element_type | solution.py:411
  2.5 60.9 %shard_map.41 = (bf16[2,6144,128]{2,1,0:T(8,128)(2,1)}, f32[16,1,1536]{2,1,0:T(1,128)}, bf16[2,1536,128]{2,1,0:T(8,128)(2,1)}) custom-call(bf16[3072,1536]{1,0:T(8,128)(2,1)} %e_ref.1, bf16[1536,128]{1,0:T(8,128)(2,1)} %convert_element_type.3.b_ref), custom_call_target="tpu_custom_call" | custom-call | tf_op jit(solution)/shard_map/pallas_call | solution.py:386
  63.4 53.5 %shard_map.42.b_ref = f32[1536,256]{1,0:T(8,128)} custom-call(bf16[2,3,4,512,128]{4,3,2,1,0:T(8,128)(2,1)} %bitcast.1, f32[16,1,1536]{2,1,0:T(1,128)} %get-tuple-element.5.s_ref, bf16[2,1536,128]{2,1,0:T(8,128)(2,1)} %get-tuple-element.7.b_ref), custom_call_target="tpu_custom_call" | custom-call | tf_op jit(solution)/shard_map/pallas_call | solution.py:136
  117.0 10.1 %shard_map.43 = (bf16[3072,128]{1,0:T(8,128)(2,1)}, f32[1536,128]{1,0:T(8,128)}) custom-call(bf16[3072,1536]{1,0:T(8,128)(2,1)} %e_ref.1, f32[16,1,1536]{2,1,0:T(1,128)} %get-tuple-element.5.s_ref, f32[1536,256]{1,0:T(8,128)} %shard_map.42.b_ref), custom_call_target="tpu_custom_call" | custom-call | tf_op jit(solution)/shard_map/pallas_call | solution.py:173
